TPU v7x, 32 devices: a whole 2x2x4 slice. The times are simulated.
32 devices in a mesh: parts: 2 (over x), space: 16 (over z, y, core).
Axes of the slice: x: 2, y: 2, z: 4, core: 2. Of those that a mesh axis runs over, the one named last changes fastest.
Arguments:
- state: float32 [66, 64, 8, 256], P('parts', 'space'), parts along dimension 0, may hold values from 0.25 to 6.5
- adjoint: float32 [64, 64, 8, 256], P('parts', 'space'), parts along dimension 0, may hold values from -6 to 6
- control: float32 [64, 64, 8, 256], P('parts', 'space'), parts along dimension 0, may hold values from -6 to 6
- target: float32 [64, 128], P('parts'), parts along dimension 0, may hold values from 1 to 3
- mask: int32 [64, 16], P('space', 'parts'), parts along dimension 1, may hold values 0 or 1
- regions: int32 [64, 16, 256], P('space', 'parts'), parts along dimension 1, may hold values from 0 to 127, as said below
Outputs:
- state_spectrum: float32 [2, 64, 64, 8, 256], P(None, 'parts', 'space'), parts along dimension 1
- adjoint_spectrum: float32 [2, 64, 64, 8, 256], P(None, 'parts', 'space'), parts along dimension 1
- gradient_residual: float32 [64, 64, 8, 256], P('parts', 'space'), parts along dimension 0
There are 2 independent parts, one for each index of `parts`. A program takes and returns all parts, laid end to end along the dimension named above; each array names one. Nothing has to cross between parts.
Inputs may be any that keep to these rules, and one draw needn't show every extreme that they name: `regions`: every region number from 0 to 127 labels at least one cell.
All inputs are finite; a program needn't handle non-finite values. No bound on the sum of `mask` on one device may be relied on, other than what follows from the above.
Results may differ from a plain program's by a relative error of at most 0.000098.
Values sent between devices are 32-bit elements; how exact they have to be, the bound alone decides.
A program may use at most 64 MiB of HBM per device.

v0:
```python
import functools
import math

import jax
import jax.numpy as jnp
from jax import lax
from jax.experimental import pallas as pl
from jax.experimental.pallas import tpu as pltpu
from jax.sharding import PartitionSpec as P

time_step = 0.15
penalty = 0.5
MESH = pl.DeviceIdType.MESH
HBM = pl.BlockSpec(memory_space=pltpu.HBM)


def real_transform(values):
    n = len(values)
    if n == 1:
        return [values[0]], [None]
    if n % 2:
        real, imag = [], []
        for k in range(n // 2 + 1):
            angles = [2.0 * math.pi * (j * k % n) / n for j in range(n)]
            real.append(sum(v * math.cos(a) for v, a in zip(values, angles)))
            imag.append(None if k == 0 else sum(v * -math.sin(a) for v, a in zip(values, angles)))
        return real, imag
    even_re, even_im = real_transform(values[::2])
    odd_re, odd_im = real_transform(values[1::2])
    m = n // 2
    real, imag = [None] * (m + 1), [None] * (m + 1)
    for k in range(m // 2 + 1):
        a_re, a_im, b_re, b_im = even_re[k], even_im[k], odd_re[k], odd_im[k]
        if k == 0:
            real[0], real[m] = a_re + b_re, a_re - b_re
            continue
        if 2 * k == m:
            real[k], imag[k] = a_re, -b_re
            continue
        c, s = math.cos(2.0 * math.pi * k / n), math.sin(2.0 * math.pi * k / n)
        t_re, t_im = c * b_re + s * b_im, c * b_im - s * b_re
        real[k], imag[k] = a_re + t_re, a_im + t_im
        real[m - k], imag[m - k] = a_re - t_re, t_im - a_im
    return real, imag


def write_spectrum(buffer, row, lanes, real, imag, n):
    zero = jnp.zeros_like(real[0])
    for k in range(n):
        low = min(k, n - k)
        buffer[0, row, k, :, lanes] = real[low]
        value = imag[low]
        buffer[1, row, k, :, lanes] = zero if value is None else (value if k == low else -value)


def pack(real, imag):
    return real + [value for value in imag if value is not None]


def solve_kernel(
    count, state, adjoint, control, regions, target, mask,
    state_buffer, packed, gradient, table, labels,
    sampled, held, multipliers, heat, wanted, allowed, residual, partial, paired, joined, crossed, summed, gathered,
    small_sem, sample_sem, held_sem, mult_sem, heat_sem,
    halo_send, halo_recv, pair_send, pair_recv, chain_send, chain_recv,
):
    steps, rows, planes, width = control.shape
    count_regions = target.shape[1]
    blocks = width // 128
    links = count // 4
    me = lax.axis_index("space")
    link, place = me // 4, me % 4
    above, below = (me + 1) % count, (me + count - 1) % count
    partner = (me // 2) * 2 + 1 - me % 2
    across = link * 4 + (place + 2) % 4
    peers = [((link + d) % links) * 4 + place for d in range(1, links)]

    barrier = pltpu.get_barrier_semaphore()

    def greet(other):
        pl.semaphore_signal(barrier, inc=1, device_id={"space": other}, device_id_type=MESH)

    for other in [above, below, across] + peers:
        greet(other)

    sums_loads = [pltpu.make_async_copy(regions, labels, small_sem.at[0])] + [
        pltpu.make_async_copy(
            state.at[pl.ds(1, steps), :, :, pl.ds(block * 128, 128)],
            sampled.at[block], sample_sem.at[block],
        )
        for block in range(blocks)
    ]
    small_loads = [
        pltpu.make_async_copy(target, wanted, small_sem.at[1]),
        pltpu.make_async_copy(mask, allowed, small_sem.at[2]),
    ]
    heat_loads, mult_loads, held_loads = [], [], []
    for y in range(rows):
        heat_loads.append(pltpu.make_async_copy(control.at[pl.ds(0, steps), y], heat.at[y], heat_sem.at[y]))
        mult_loads.append(
            pltpu.make_async_copy(adjoint.at[pl.ds(0, steps), y], multipliers.at[y + 1], mult_sem.at[y])
        )
        held_loads.append(
            pltpu.make_async_copy(state.at[pl.ds(0, steps + 1), y], held.at[y + 1], held_sem.at[y])
        )
    for load in sums_loads + small_loads + heat_loads + mult_loads + held_loads:
        load.start()

    copies = []
    for source, first, target_rows, shift, length in (
        (state, 0, held, 0, steps), (adjoint, 1, multipliers, 1, steps - 1),
    ):
        for block in range(blocks):
            lanes = pl.ds(block * 128, 128)
            for row, into, other in ((rows - 1, 0, above), (0, rows + 1, below)):
                n = len(copies)
                copies.append(
                    pltpu.make_async_remote_copy(
                        src_ref=source.at[pl.ds(first, length), row, :, lanes],
                        dst_ref=target_rows.at[into, pl.ds(shift, length), :, lanes],
                        send_sem=halo_send.at[n],
                        recv_sem=halo_recv.at[n],
                        device_id={"space": other},
                        device_id_type=MESH,
                    )
                )

    flat = sampled.reshape(blocks, steps * rows * planes, 128)
    region_ids = lax.broadcasted_iota(jnp.int32, (count_regions, width), 0)

    def add_row(row, total):
        values = jnp.concatenate(
            [
                flat[block, pl.ds(row * planes + plane, steps, stride=rows * planes), :]
                for plane in range(planes)
                for block in range(blocks)
            ],
            axis=1,
        )
        high = values.astype(jnp.bfloat16)
        low = (values - high.astype(jnp.float32)).astype(jnp.bfloat16)
        ones = jnp.ones((16, planes * width), jnp.bfloat16)
        stacked = jnp.concatenate([high, low, ones], axis=0)
        onehot = jnp.concatenate(
            [
                (labels[row, pl.ds(plane, 1), :] == region_ids).astype(jnp.float32).astype(jnp.bfloat16)
                for plane in range(planes)
            ],
            axis=1,
        )
        return total + lax.dot_general(
            stacked, onehot, (((1,), (1,)), ((), ())), preferred_element_type=jnp.float32
        )

    pl.semaphore_wait(barrier, 3 + len(peers))
    for copy in copies[:2]:
        copy.start()
    for load in sums_loads:
        load.wait()
    total = jnp.zeros((2 * steps + 16, count_regions), jnp.float32)
    total = lax.fori_loop(0, rows, add_row, total)
    partial[:steps] = total[:steps] + total[steps : 2 * steps]
    partial[steps:] = total[2 * steps : 2 * steps + 8]
    pair = pltpu.make_async_remote_copy(
        src_ref=partial, dst_ref=paired, send_sem=pair_send.at[0], recv_sem=pair_recv.at[0],
        device_id={"space": partner}, device_id_type=MESH,
    )
    pair.start()

    lane = lax.broadcasted_iota(jnp.int32, (planes, width), 1)
    plane_ids = lax.broadcasted_iota(jnp.int32, (planes, width), 0)
    first_lane, last_lane = lane == 0, lane == width - 1
    first_plane, last_plane = plane_ids == 0, plane_ids == planes - 1

    def support_of(y):
        support = jnp.zeros((planes, width), jnp.float32)
        for plane in range(planes):
            support = jnp.where(plane_ids == plane, allowed[y, plane].astype(jnp.float32), support)
        return support

    for load in small_loads + heat_loads + mult_loads:
        load.wait()

    def gradient_row(y, carry):
        support = support_of(y)

        def step(j, inner):
            gradient[y, j] = penalty * heat[y, j] - support * multipliers[y + 1, j]
            return inner

        return lax.fori_loop(0, steps, step, carry, unroll=True)

    lax.fori_loop(0, rows, gradient_row, 0)

    pair.wait()
    joined[...] = partial[...] + paired[...]
    cross = pltpu.make_async_remote_copy(
        src_ref=joined, dst_ref=crossed, send_sem=pair_send.at[1], recv_sem=pair_recv.at[1],
        device_id={"space": across}, device_id_type=MESH,
    )
    cross.start()
    for copy in copies[2:4]:
        copy.start()

    sends = [
        pltpu.make_async_remote_copy(
            src_ref=summed, dst_ref=gathered.at[d], send_sem=chain_send.at[d], recv_sem=chain_recv.at[d],
            device_id={"space": peer}, device_id_type=MESH,
        )
        for d, peer in enumerate(peers)
    ]

    def laplace(values, beside):
        total = beside + jnp.where(first_lane, 0.0, pltpu.roll(values, 1, 1))
        total = total + jnp.where(last_lane, 0.0, pltpu.roll(values, width - 1, 1))
        total = total + jnp.where(first_plane, 0.0, pltpu.roll(values, 1, 0))
        total = total + jnp.where(last_plane, 0.0, pltpu.roll(values, planes - 1, 0))
        return total - 6.0 * values

    def adjoint_transform(y, beside):
        def step(j, carry):
            later = multipliers[y + 1, j + 1]
            residual[j] = multipliers[y + 1, j] - later - time_step * laplace(later, beside(j + 1))
            return carry

        lax.fori_loop(0, steps - 1, step, 0, unroll=True)
        residual[steps - 1] = multipliers[y + 1, steps - 1]
        for block in range(blocks):
            lanes = pl.ds(block * 128, 128)
            values = real_transform([residual[j, :, lanes] for j in range(steps)])
            for k, value in enumerate(pack(*values)):
                packed[y, k, :, lanes] = value

    def adjoint_inner(y, carry):
        adjoint_transform(y, lambda j: multipliers[y, j] + multipliers[y + 2, j])
        return carry

    def adjoint_edge(side, carry):
        adjoint_transform(side * (rows - 1), lambda j: multipliers[2 + side * (rows - 3), j])
        return carry

    def state_row(y, carry):
        support = support_of(y)

        def step(j, inner):
            now = held[y + 1, j]
            lap = laplace(now, held[y, j] + held[y + 2, j])
            residual[j] = held[y + 1, j + 1] - now - time_step * lap - time_step * support * heat[y, j]
            return inner

        lax.fori_loop(0, steps, step, 0, unroll=True)
        for block in range(blocks):
            lanes = pl.ds(block * 128, 128)
            real, imag = real_transform([residual[j, :, lanes] for j in range(steps)])
            write_spectrum(state_buffer, y, lanes, real, imag, steps)
        return carry

    lax.fori_loop(1, rows - 1, adjoint_inner, 0)
    cross.wait()
    summed[...] = joined[...] + crossed[...]
    for send in sends:
        send.start()
    for copy in copies[4:]:
        copy.start()
    lax.fori_loop(0, 2, adjoint_edge, 0)
    for load in held_loads:
        load.wait()
    lax.fori_loop(1, rows - 1, state_row, 0)
    for copy in copies[: 2 * blocks]:
        copy.wait()
    lax.fori_loop(0, 2, lambda side, carry: state_row(side * (rows - 1), carry), 0)

    result = summed[...]
    for d, send in enumerate(sends):
        send.wait()
        result = result + gathered[d]
    misfit = result[:steps] / result[steps : steps + 1] - wanted[...]
    values = real_transform(
        [jnp.broadcast_to(misfit[j : j + 1], (8, count_regions)) for j in range(steps)]
    )
    for k, value in enumerate(pack(*values)):
        table[k] = value

    for block in range(blocks):
        lanes = pl.ds(block * 128, 128)
        for side in range(2):
            copies[2 * (blocks + block) + side].wait()

        def add_halo(side, carry):
            y, outer = side * (rows - 1), side * (rows + 1)
            values = [-time_step * multipliers[outer, j + 1, :, lanes] for j in range(steps - 1)]
            values.append(jnp.zeros_like(values[0]))
            for k, value in enumerate(pack(*real_transform(values))):
                packed[y, k, :, lanes] += value
            return carry

        lax.fori_loop(0, 2, add_halo, 0)


def solve(count, state, adjoint, control, regions, target, mask):
    steps, rows, planes, width = control.shape
    count_regions = target.shape[1]
    padded = (steps + 8, count_regions)
    blocks = width // 128
    f32, dma, vmem = jnp.float32, pltpu.SemaphoreType.DMA, pltpu.VMEM
    in_vmem = pl.BlockSpec(memory_space=pltpu.VMEM)
    return pl.pallas_call(
        functools.partial(solve_kernel, count),
        out_shape=(
            vmem((2, rows, steps, planes, width), f32),
            vmem((rows, steps, planes, width), f32),
            vmem((rows, steps, planes, width), f32),
            vmem((steps, 8, count_regions), f32),
            vmem(regions.shape, jnp.int32),
        ),
        in_specs=[HBM] * 6,
        out_specs=(in_vmem,) * 5,
        scratch_shapes=[
            vmem((blocks, steps, rows, planes, 128), f32),
            vmem((rows + 2, steps + 1, planes, width), f32),
            vmem((rows + 2, steps, planes, width), f32),
            vmem((rows, steps, planes, width), f32),
            vmem(target.shape, f32),
            pltpu.SMEM(mask.shape, jnp.int32),
            vmem((steps, planes, width), f32),
        ]
        + [vmem(padded, f32)] * 5
        + [
            vmem((count // 4 - 1,) + padded, f32),
            dma((3,)),
            dma((blocks,)),
            dma((rows,)),
            dma((rows,)),
            dma((rows,)),
            dma((4 * blocks,)),
            dma((4 * blocks,)),
            dma((2,)),
            dma((2,)),
            dma((count // 4 - 1,)),
            dma((count // 4 - 1,)),
        ],
        compiler_params=pltpu.CompilerParams(
            collective_id=0, has_side_effects=True, vmem_limit_bytes=24 * 2**20
        ),
        name="solve",
    )(state, adjoint, control, regions, target, mask)


def finish_kernel(
    state_buffer, packed, gradient, table, labels,
    state_out, adjoint_out, gradient_out,
    adjoint_buffer, state_sem, adjoint_sem, gradient_sem,
):
    rows, steps, planes, width = gradient.shape
    early = []
    for y in range(rows):
        for part in range(2):
            early.append(
                pltpu.make_async_copy(
                    state_buffer.at[part, y], state_out.at[part, pl.ds(0, steps), y], state_sem.at[part, y]
                )
            )
        early.append(
            pltpu.make_async_copy(gradient.at[y], gradient_out.at[pl.ds(0, steps), y], gradient_sem.at[y])
        )
    for copy in early:
        copy.start()

    def outputs(y):
        return [
            pltpu.make_async_copy(
                adjoint_buffer.at[part, y], adjoint_out.at[part, pl.ds(0, steps), y], adjoint_sem.at[part, y]
            )
            for part in range(2)
        ]

    def row_body(y, carry):
        for block in range(width // 128):
            lanes = pl.ds(block * 128, 128)
            ids = labels[y, :, lanes]
            values = [
                packed[y, k, :, lanes] + jnp.take_along_axis(table[k], ids, axis=1, mode="promise_in_bounds")
                for k in range(steps)
            ]
            top = steps // 2 + 1
            imag = [None] + values[top:] + [None] * (2 * top - 1 - steps)
            write_spectrum(adjoint_buffer, y, lanes, values[:top], imag, steps)
        for copy in outputs(y):
            copy.start()
        return carry

    lax.fori_loop(0, rows, row_body, 0)
    for copy in early + [copy for y in range(rows) for copy in outputs(y)]:
        copy.wait()


def finish(control, state_buffer, packed, gradient, table, labels):
    steps, rows, planes, width = control.shape
    f32, dma = jnp.float32, pltpu.SemaphoreType.DMA
    in_vmem = pl.BlockSpec(memory_space=pltpu.VMEM)
    spectrum_shape = jax.ShapeDtypeStruct((2,) + control.shape, f32)
    return pl.pallas_call(
        finish_kernel,
        out_shape=(spectrum_shape, spectrum_shape, jax.ShapeDtypeStruct(control.shape, f32)),
        in_specs=[in_vmem] * 5,
        out_specs=(HBM,) * 3,
        scratch_shapes=[
            pltpu.VMEM((2, rows, steps, planes, width), f32),
            dma((2, rows)),
            dma((2, rows)),
            dma((rows,)),
        ],
        compiler_params=pltpu.CompilerParams(vmem_limit_bytes=16 * 2**20),
        name="finish",
    )(state_buffer, packed, gradient, table, labels)


def on_device(count, *arrays):
    state, adjoint, control, target, mask, regions = (
        pltpu.with_memory_space_constraint(array, pltpu.HBM) for array in arrays
    )
    found = solve(count, state, adjoint, control, regions, target, mask)
    return finish(control, *found)


def solution(mesh):
    return jax.shard_map(
        functools.partial(on_device, mesh.shape["space"]),
        mesh=mesh,
        in_specs=(
            P("parts", "space", None, None),
            P("parts", "space", None, None),
            P("parts", "space", None, None),
            P("parts", None),
            P("space", "parts"),
            P("space", "parts", None),
        ),
        out_specs=(
            P(None, "parts", "space", None, None),
            P(None, "parts", "space", None, None),
            P("parts", "space", None, None),
        ),
        check_vma=False,
    )
```

profile of v0, /device:TPU:1, one launch (start us, length us, event | category | flops | bytes accessed | tf_op | source)
XLA Modules:
  0.0 22.1 jit_solution(9588284228323453494)
XLA Ops:
  0.6 19.0 %solve.1 = (f32[2,4,32,8,256]{4,3,2,1,0:T(8,128)S(1)}, f32[4,32,8,256]{3,2,1,0:T(8,128)S(1)}, f32[4,32,8,256]{3,2,1,0:T(8,128)S(1)}, f32[32,8,128]{2,1,0:T(8,128)S(1)}, s32[4,8,256]{2,1,0:T(8,128)S(1)}) custom-call(f32[33,4,8,256]{3,2,1,0:T(8,128)} %state.1, f32[32,4,8,256]{3,2,1,0:T(8,128)} %adjoint.1, f32[32,4,8,256]{3,2,1,0:T(8,128)} %control.1, ...), custom_call_target="tpu_custom_call" | custom-call | tf_op jit(solution)/shard_map/solve/pallas_call | solution.py:307
  19.6 2.5 %finish.1 = (f32[2,32,4,8,256]{4,3,2,1,0:T(8,128)}, f32[2,32,4,8,256]{4,3,2,1,0:T(8,128)}, f32[32,4,8,256]{3,2,1,0:T(8,128)}) custom-call(f32[2,4,32,8,256]{4,3,2,1,0:T(8,128)S(1)} %get-tuple-element.8.state_buffer, f32[4,32,8,256]{3,2,1,0:T(8,128)S(1)} %get-tuple-element.9.packed, f32[4,32,8,256]{3,2,1,0:T(8,128)S(1)} %get-tuple-element.10.gradient, ...), custom_call_target="tpu_custom_call" | custom-call | tf_op jit(solution)/shard_map/finish/pallas_call | solution.py:402
where the time goes:
time: 22.3 us; the launch traced here: 22.1 us
  Pallas kernels  21.5 us (96%)
  between operations  0.64 us (3%)
    pallas_call x1, Pallas kernels, solve(): pl.pallas_call(functools.partial(solve_kernel, count), out_shape=(vmem((2...  19 us
    pallas_call x1, Pallas kernels, finish(): pl.pallas_call(finish_kernel, out_shape=(spectrum_shape, spectrum_shape,...  2.49 us

commit v1 on v0

v1 whole, which is shorter than its diff:
```python
import functools
import math

import jax
import jax.numpy as jnp
from jax import lax
from jax.experimental import pallas as pl
from jax.experimental.pallas import tpu as pltpu
from jax.sharding import PartitionSpec as P

time_step = 0.15
penalty = 0.5
MESH = pl.DeviceIdType.MESH
HBM = pl.BlockSpec(memory_space=pltpu.HBM)


def real_transform(values):
    n = len(values)
    if n == 1:
        return [values[0]], [None]
    if n % 2:
        real, imag = [], []
        for k in range(n // 2 + 1):
            angles = [2.0 * math.pi * (j * k % n) / n for j in range(n)]
            real.append(sum(v * math.cos(a) for v, a in zip(values, angles)))
            imag.append(None if k == 0 else sum(v * -math.sin(a) for v, a in zip(values, angles)))
        return real, imag
    even_re, even_im = real_transform(values[::2])
    odd_re, odd_im = real_transform(values[1::2])
    m = n // 2
    real, imag = [None] * (m + 1), [None] * (m + 1)
    for k in range(m // 2 + 1):
        a_re, a_im, b_re, b_im = even_re[k], even_im[k], odd_re[k], odd_im[k]
        if k == 0:
            real[0], real[m] = a_re + b_re, a_re - b_re
            continue
        if 2 * k == m:
            real[k], imag[k] = a_re, -b_re
            continue
        c, s = math.cos(2.0 * math.pi * k / n), math.sin(2.0 * math.pi * k / n)
        t_re, t_im = c * b_re + s * b_im, c * b_im - s * b_re
        real[k], imag[k] = a_re + t_re, a_im + t_im
        real[m - k], imag[m - k] = a_re - t_re, t_im - a_im
    return real, imag


def write_spectrum(put, real, imag, n):
    zero = jnp.zeros_like(real[0])
    for k in range(n):
        low = min(k, n - k)
        put(0, k, real[low])
        value = imag[low]
        put(1, k, zero if value is None else (value if k == low else -value))


def pack(real, imag):
    return real + [value for value in imag if value is not None]


def solve_kernel(
    count, state, adjoint, control, regions, target, mask,
    state_buffer, packed, gradient, misfit, labels,
    sampled, held, multipliers, heat, wanted, allowed, residual, partial, paired, joined, crossed, summed, total, gathered,
    load_sem, ready, near_send, near_recv, far_send, far_recv, sum_send, sum_recv, chain_sem,
):
    steps, rows, planes, width = control.shape
    count_regions = target.shape[1]
    blocks = width // 128
    links = count // 4
    me = lax.axis_index("space")
    link, place = me // 4, me % 4
    odd = me % 2
    partner = me + 1 - 2 * odd
    outside = (me + count - 1 + 2 * odd) % count
    hub = (place == 0) | (place == 3)
    last = me == count - 1
    origin = me == 0
    mate = link * 4 + 3 - place
    peers = [((link + d) % links) * 4 + place for d in range(1, links)]
    near_row, far_row = (1 - odd) * (rows - 1), odd * (rows - 1)
    near_halo, far_halo = (1 - odd) * (rows + 1), odd * (rows + 1)

    barrier = pltpu.get_barrier_semaphore()

    def greet(other):
        pl.semaphore_signal(barrier, inc=1, device_id={"space": other}, device_id_type=MESH)

    greet(partner)
    greet(outside)

    @pl.when(hub)
    def _():
        for other in [mate] + peers:
            greet(other)

    label_load = pltpu.make_async_copy(regions, labels, load_sem.at[0])

    def local(source, into, sem):
        return pltpu.make_async_copy(source, into, sem)

    sample_loads = [
        local(state.at[pl.ds(1, steps), y, plane], sampled.at[y, plane], load_sem.at[1])
        for y in range(rows)
        for plane in range(planes)
    ]
    later_loads = [local(target, wanted, load_sem.at[2]), local(mask, allowed, load_sem.at[3])]
    own = pl.ds(1, rows)
    for y in range(rows):
        later_loads += [
            local(adjoint.at[pl.ds(0, steps), y], multipliers.at[y + 1], load_sem.at[4]),
            local(control.at[pl.ds(0, steps), y], heat.at[y], load_sem.at[5]),
            local(state.at[pl.ds(0, steps + 1), y], held.at[y + 1], load_sem.at[6]),
        ]
    def arrive(ref, sem):
        local(ref, ref, sem).wait()

    near_copies, far_copies = [], []
    for source, first, target_rows, shift, length in (
        (state, 0, held, 0, steps), (adjoint, 1, multipliers, 1, steps - 1),
    ):
        n = len(near_copies)
        near_copies.append(
            pltpu.make_async_remote_copy(
                src_ref=source.at[pl.ds(first, length), near_row],
                dst_ref=target_rows.at[odd * (rows + 1), pl.ds(shift, length)],
                send_sem=near_send.at[n],
                recv_sem=near_recv.at[n],
                device_id={"space": partner},
                device_id_type=MESH,
            )
        )
        for block in range(blocks):
            lanes = pl.ds(block * 128, 128)
            n = len(far_copies)
            far_copies.append(
                pltpu.make_async_remote_copy(
                    src_ref=source.at[pl.ds(first, length), far_row, :, lanes],
                    dst_ref=target_rows.at[(1 - odd) * (rows + 1), pl.ds(shift, length), :, lanes],
                    send_sem=far_send.at[n // blocks],
                    recv_sem=far_recv.at[max(n - blocks + 1, 0)],
                    device_id={"space": outside},
                    device_id_type=MESH,
                )
            )

    def message(n, source, into, other):
        return pltpu.make_async_remote_copy(
            src_ref=source, dst_ref=into, send_sem=sum_send.at[n], recv_sem=sum_recv.at[n],
            device_id={"space": other}, device_id_type=MESH,
        )

    gather_sums = message(0, partial, paired, partner)
    cross_sums = message(1, joined, crossed, mate)
    share_sums = message(2, total, total, partner)
    chain_sums = [
        pltpu.make_async_remote_copy(
            src_ref=summed, dst_ref=gathered.at[d], send_sem=chain_sem.at[0], recv_sem=chain_sem.at[1],
            device_id={"space": peer}, device_id_type=MESH,
        )
        for d, peer in enumerate(peers)
    ]

    region_ids = lax.broadcasted_iota(jnp.int32, (count_regions, width), 0).astype(jnp.float32).astype(jnp.bfloat16)
    yes = jnp.ones((count_regions, width), jnp.bfloat16)
    no = jnp.zeros((count_regions, width), jnp.bfloat16)

    def add_row(row, carry):
        values = jnp.concatenate([sampled[row, plane] for plane in range(planes)], axis=1)
        high = values.astype(jnp.bfloat16)
        low = (values - high.astype(jnp.float32)).astype(jnp.bfloat16)
        ones = jnp.ones((16, planes * width), jnp.bfloat16)
        stacked = jnp.concatenate([high, low, ones], axis=0)
        onehot = jnp.concatenate(
            [
                jnp.where(
                    labels[row, pl.ds(plane, 1), :].astype(jnp.float32).astype(jnp.bfloat16) == region_ids, yes, no
                )
                for plane in range(planes)
            ],
            axis=1,
        )
        return carry + lax.dot_general(
            stacked, onehot, (((1,), (1,)), ((), ())), preferred_element_type=jnp.float32
        )

    def meet():
        pl.semaphore_wait(barrier, 2)
        for copy in far_copies:
            copy.start()
        pl.semaphore_signal(ready, inc=1, device_id={"space": outside}, device_id_type=MESH)

    pl.when(place == 2)(meet)
    label_load.start()
    for load in sample_loads:
        load.start()
    pl.when(place == 1)(meet)

    label_load.wait()
    arrive(sampled, load_sem.at[1])
    found = jnp.zeros((2 * steps + 16, count_regions), jnp.float32)
    for y in range(rows):
        found = add_row(y, found)
    partial[:steps] = found[:steps] + found[steps : 2 * steps]
    partial[steps:] = found[2 * steps : 2 * steps + 8]

    @pl.when(jnp.logical_not(hub))
    def _():
        pl.semaphore_wait(ready, 1)
        gather_sums.start()
        for copy in near_copies:
            copy.start()
        arrive(held.at[far_halo, pl.ds(0, steps)], far_send.at[0])

    for load in later_loads:
        load.start()

    @pl.when(last)
    def _():
        pl.semaphore_wait(barrier, 3 + len(peers))
        for copy in far_copies:
            copy.start()

    @pl.when(hub)
    def _():
        gather_sums.wait_recv()
        joined[...] = partial[...] + paired[...]
        cross_sums.start()
        for copy in near_copies:
            copy.start()

        @pl.when(jnp.logical_not(last | origin))
        def _():
            pl.semaphore_wait(barrier, 3 + len(peers))

        @pl.when((place == 0) & jnp.logical_not(origin))
        def _():
            for copy in far_copies[:blocks]:
                copy.start()

    lane = lax.broadcasted_iota(jnp.int32, (planes, width), 1)
    plane_ids = lax.broadcasted_iota(jnp.int32, (planes, width), 0)
    first_lane, last_lane = lane == 0, lane == width - 1
    first_plane, last_plane = plane_ids == 0, plane_ids == planes - 1

    def support_of(y):
        support = jnp.zeros((planes, width), jnp.float32)
        for plane in range(planes):
            support = jnp.where(plane_ids == plane, allowed[y, plane].astype(jnp.float32), support)
        return support

    def laplace(values, beside):
        total = beside + jnp.where(first_lane, 0.0, pltpu.roll(values, 1, 1))
        total = total + jnp.where(last_lane, 0.0, pltpu.roll(values, width - 1, 1))
        total = total + jnp.where(first_plane, 0.0, pltpu.roll(values, 1, 0))
        total = total + jnp.where(last_plane, 0.0, pltpu.roll(values, planes - 1, 0))
        return total - 6.0 * values

    def adjoint_transform(y, beside):
        def step(j, carry):
            later = multipliers[y + 1, j + 1]
            residual[j] = multipliers[y + 1, j] - later - time_step * laplace(later, beside(j + 1))
            return carry

        lax.fori_loop(0, steps - 1, step, 0, unroll=True)
        residual[steps - 1] = multipliers[y + 1, steps - 1]
        for block in range(blocks):
            lanes = pl.ds(block * 128, 128)
            values = real_transform([residual[j, :, lanes] for j in range(steps)])
            for k, value in enumerate(pack(*values)):
                packed[y, k, :, lanes] = value

    def adjoint_full(y, carry):
        adjoint_transform(y, lambda j: multipliers[y, j] + multipliers[y + 2, j])
        return carry

    def state_row(y, carry):
        support = support_of(y)

        def step(j, inner):
            now = held[y + 1, j]
            lap = laplace(now, held[y, j] + held[y + 2, j])
            residual[j] = held[y + 1, j + 1] - now - time_step * lap - time_step * support * heat[y, j]
            return inner

        lax.fori_loop(0, steps, step, 0, unroll=True)
        for block in range(blocks):
            lanes = pl.ds(block * 128, 128)
            real, imag = real_transform([residual[j, :, lanes] for j in range(steps)])

            def put(part, k, value):
                state_buffer[part, k, y, :, lanes] = value

            write_spectrum(put, real, imag, steps)
        return carry

    def gradient_row(y, carry):
        support = support_of(y)

        def step(j, inner):
            gradient[j, y] = penalty * heat[y, j] - support * multipliers[y + 1, j]
            return inner

        return lax.fori_loop(0, steps, step, carry, unroll=True)

    for load in later_loads[:2]:
        load.wait()
    arrive(multipliers.at[own], load_sem.at[4])

    lax.fori_loop(1, rows - 1, adjoint_full, 0)

    adjoint_transform(far_row, lambda j: multipliers[far_row + 2 - 2 * odd, j])

    arrive(heat, load_sem.at[5])
    arrive(held.at[own], load_sem.at[6])

    lax.fori_loop(0, rows, gradient_row, 0)

    @pl.when(origin)
    def _():
        pl.semaphore_wait(barrier, 3 + len(peers))
        far_copies[0].start()

    @pl.when(hub)
    def _():
        cross_sums.wait()
        summed[...] = joined[...] + crossed[...]
        for send in chain_sums:
            send.start()

        @pl.when(jnp.logical_not(last | origin))
        def _():
            @pl.when(place == 3)
            def _():
                for copy in far_copies[:blocks]:
                    copy.start()

            for copy in far_copies[blocks:]:
                copy.start()

    lax.fori_loop(1, rows - 1, state_row, 0)

    for copy in near_copies:
        copy.wait()
    lax.fori_loop(near_row, near_row + 1, adjoint_full, 0)
    lax.fori_loop(near_row, near_row + 1, state_row, 0)

    @pl.when(origin)
    def _():
        for copy in far_copies[1:]:
            copy.start()

    @pl.when(hub)
    def _():
        result = summed[...]
        arrive(gathered, chain_sem.at[1])
        for d in range(len(peers)):
            result = result + gathered[d]
        total[...] = result
        share_sums.start()

    arrive(held.at[far_halo, pl.ds(0, steps)], far_recv.at[0])
    lax.fori_loop(far_row, far_row + 1, state_row, 0)

    def add_far(block):
        lanes = pl.ds(block * 128, 128)
        far_copies[blocks + block].wait_recv()

        values = [-time_step * multipliers[far_halo, j + 1, :, lanes] for j in range(steps - 1)]
        values.append(jnp.zeros_like(values[0]))
        for k, value in enumerate(pack(*real_transform(values))):
            packed[far_row, k, :, lanes] += value

    for block in range(blocks - 1):
        add_far(block)

    @pl.when(jnp.logical_not(hub))
    def _():
        gather_sums.wait_send()
        share_sums.wait_recv()

    misfit[...] = total[:steps] / total[steps : steps + 1] - wanted[...]
    add_far(blocks - 1)

    arrive(multipliers.at[far_halo, pl.ds(1, steps - 1)], far_send.at[1])

    @pl.when(hub)
    def _():
        arrive(held.at[far_halo, pl.ds(0, steps)], far_send.at[0])
        arrive(gathered, chain_sem.at[0])
        share_sums.wait_send()


def solve(count, state, adjoint, control, regions, target, mask):
    steps, rows, planes, width = control.shape
    count_regions = target.shape[1]
    padded = (steps + 8, count_regions)
    blocks = width // 128
    f32, dma, vmem = jnp.float32, pltpu.SemaphoreType.DMA, pltpu.VMEM
    in_vmem = pl.BlockSpec(memory_space=pltpu.VMEM)
    return pl.pallas_call(
        functools.partial(solve_kernel, count),
        out_shape=(
            vmem((2,) + control.shape, f32),
            vmem((rows, steps, planes, width), f32),
            vmem(control.shape, f32),
            vmem(target.shape, f32),
            vmem(regions.shape, jnp.int32),
        ),
        in_specs=[HBM] * 6,
        out_specs=(in_vmem,) * 5,
        scratch_shapes=[
            vmem((rows, planes, steps, width), f32),
            vmem((rows + 2, steps + 1, planes, width), f32),
            vmem((rows + 2, steps, planes, width), f32),
            vmem((rows, steps, planes, width), f32),
            vmem(target.shape, f32),
            pltpu.SMEM(mask.shape, jnp.int32),
            vmem((steps, planes, width), f32),
        ]
        + [vmem(padded, f32)] * 6
        + [
            vmem((count // 4 - 1,) + padded, f32),
            dma((7,)),
            pltpu.SemaphoreType.REGULAR,
            dma((2,)),
            dma((2,)),
            dma((2,)),
            dma((1 + blocks,)),
            dma((3,)),
            dma((3,)),
            dma((2,)),
        ],
        compiler_params=pltpu.CompilerParams(
            collective_id=0, has_side_effects=True, vmem_limit_bytes=24 * 2**20
        ),
        name="solve",
    )(state, adjoint, control, regions, target, mask)


def finish_kernel(
    state_buffer, packed, gradient, misfit, labels,
    state_out, adjoint_out, gradient_out,
    adjoint_buffer, table, out_sem,
):
    steps, rows, planes, width = gradient.shape
    writes = [
        pltpu.make_async_copy(state_buffer, state_out, out_sem.at[0]),
        pltpu.make_async_copy(gradient, gradient_out, out_sem.at[1]),
    ]
    for write in writes:
        write.start()

    values = real_transform([jnp.broadcast_to(misfit[j : j + 1], (8, table.shape[2])) for j in range(steps)])
    for k, value in enumerate(pack(*values)):
        table[k] = value

    def row_body(y, carry):
        for block in range(width // 128):
            lanes = pl.ds(block * 128, 128)
            ids = labels[y, :, lanes]
            values = [
                packed[y, k, :, lanes] + jnp.take_along_axis(table[k], ids, axis=1, mode="promise_in_bounds")
                for k in range(steps)
            ]
            top = steps // 2 + 1
            imag = [None] + values[top:] + [None] * (2 * top - 1 - steps)

            def put(part, k, value):
                adjoint_buffer[part, y, k, :, lanes] = value

            write_spectrum(put, values[:top], imag, steps)
        for part in range(2):
            pltpu.make_async_copy(
                adjoint_buffer.at[part, y], adjoint_out.at[part, pl.ds(0, steps), y], out_sem.at[2]
            ).start()
        return carry

    lax.fori_loop(0, rows, row_body, 0)
    for write in writes:
        write.wait()
    pltpu.make_async_copy(adjoint_buffer, adjoint_buffer, out_sem.at[2]).wait()


def finish(control, state_buffer, packed, gradient, misfit, labels):
    steps, rows, planes, width = control.shape
    f32, dma = jnp.float32, pltpu.SemaphoreType.DMA
    in_vmem = pl.BlockSpec(memory_space=pltpu.VMEM)
    spectrum_shape = jax.ShapeDtypeStruct((2,) + control.shape, f32)
    return pl.pallas_call(
        finish_kernel,
        out_shape=(spectrum_shape, spectrum_shape, jax.ShapeDtypeStruct(control.shape, f32)),
        in_specs=[in_vmem] * 5,
        out_specs=(HBM,) * 3,
        scratch_shapes=[
            pltpu.VMEM((2, rows, steps, planes, width), f32),
            pltpu.VMEM((steps, 8, misfit.shape[1]), f32),
            dma((3,)),
        ],
        compiler_params=pltpu.CompilerParams(vmem_limit_bytes=16 * 2**20),
        name="finish",
    )(state_buffer, packed, gradient, misfit, labels)


def on_device(count, *arrays):
    state, adjoint, control, target, mask, regions = (
        pltpu.with_memory_space_constraint(array, pltpu.HBM) for array in arrays
    )
    found = solve(count, state, adjoint, control, regions, target, mask)
    return finish(control, *found)


def solution(mesh):
    return jax.shard_map(
        functools.partial(on_device, mesh.shape["space"]),
        mesh=mesh,
        in_specs=(
            P("parts", "space", None, None),
            P("parts", "space", None, None),
            P("parts", "space", None, None),
            P("parts", None),
            P("space", "parts"),
            P("space", "parts", None),
        ),
        out_specs=(
            P(None, "parts", "space", None, None),
            P(None, "parts", "space", None, None),
            P("parts", "space", None, None),
        ),
        check_vma=False,
    )
```

time: 22.3 us -> 18.9 us (0.85)
  Pallas kernels: 21.5 us -> 18.1 us
    pallas_call x1, Pallas kernels: 19 us -> 15.7 us  [solve(): pl.pallas_call(functools.partial(solve_kernel, count), out_shape=(vmem((2...]
where the time goes in v1:
time: 18.9 us; the launch traced here: 18.7 us
  Pallas kernels  18.1 us (96%)
  between operations  0.64 us (3%)
    pallas_call x1, Pallas kernels, solve(): pl.pallas_call(functools.partial(solve_kernel, count), out_shape=(vmem((2...  15.7 us
    pallas_call x1, Pallas kernels, finish(): pl.pallas_call(finish_kernel, out_shape=(spectrum_shape, spectrum_shape,...  2.35 us

profile of v1, /device:TPU:1, one launch (start us, length us, event | category | flops | bytes accessed | tf_op | source)
XLA Modules:
  0.0 18.7 jit_solution(15477684700543219616)
XLA Ops:
  0.6 15.7 %solve.1 = (f32[2,32,4,8,256]{4,3,2,1,0:T(8,128)S(1)}, f32[4,32,8,256]{3,2,1,0:T(8,128)S(1)}, f32[32,4,8,256]{3,2,1,0:T(8,128)S(1)}, f32[32,128]{1,0:T(8,128)S(1)}, s32[4,8,256]{2,1,0:T(8,128)S(1)}) custom-call(f32[33,4,8,256]{3,2,1,0:T(8,128)} %state.1, f32[32,4,8,256]{3,2,1,0:T(8,128)} %adjoint.1, f32[32,4,8,256]{3,2,1,0:T(8,128)} %control.1, ...), custom_call_target="tpu_custom_call" | custom-call | tf_op jit(solution)/shard_map/solve/pallas_call | solution.py:400
  16.3 2.3 %finish.1 = (f32[2,32,4,8,256]{4,3,2,1,0:T(8,128)}, f32[2,32,4,8,256]{4,3,2,1,0:T(8,128)}, f32[32,4,8,256]{3,2,1,0:T(8,128)}) custom-call(f32[2,32,4,8,256]{4,3,2,1,0:T(8,128)S(1)} %get-tuple-element.8.state_buffer, f32[4,32,8,256]{3,2,1,0:T(8,128)S(1)} %get-tuple-element.9.packed, f32[32,4,8,256]{3,2,1,0:T(8,128)S(1)} %get-tuple-element.10.gradient, ...), custom_call_target="tpu_custom_call" | custom-call | tf_op jit(solution)/shard_map/finish/pallas_call | solution.py:489

commit v2 on v1

--- a/solution.py
+++ b/solution.py
@@ -12,6 +12,7 @@
 penalty = 0.5
 MESH = pl.DeviceIdType.MESH
 HBM = pl.BlockSpec(memory_space=pltpu.HBM)
+RELAY_STEPS = 4
 
 
 def real_transform(values):
@@ -60,8 +61,8 @@
 def solve_kernel(
     count, state, adjoint, control, regions, target, mask,
     state_buffer, packed, gradient, misfit, labels,
-    sampled, held, multipliers, heat, wanted, allowed, residual, partial, paired, joined, crossed, summed, total, gathered,
-    load_sem, ready, near_send, near_recv, far_send, far_recv, sum_send, sum_recv, chain_sem,
+    sampled, held, multipliers, heat, wanted, allowed, residual, partial, paired, joined, crossed, summed, total, gathered, parcel,
+    load_sem, ready, near_send, near_recv, far_send, far_recv, sum_send, sum_recv, chain_sem, relay_sem,
 ):
     steps, rows, planes, width = control.shape
     count_regions = target.shape[1]
@@ -75,6 +76,11 @@
     hub = (place == 0) | (place == 3)
     last = me == count - 1
     origin = me == 0
+    relays = min(links - 1, 3)
+    carried = RELAY_STEPS
+    direct = steps - 1 - relays * carried
+    relay = (place == 0) & (link >= 1) & (link <= relays)
+    helpers = [4 * (d + 1) for d in range(relays) if d + 1 < links - 1]
     mate = link * 4 + 3 - place
     peers = [((link + d) % links) * 4 + place for d in range(1, links)]
     near_row, far_row = (1 - odd) * (rows - 1), odd * (rows - 1)
@@ -92,6 +98,10 @@
     def _():
         for other in [mate] + peers:
             greet(other)
+
+    @pl.when(relay & (link < links - 1))
+    def _():
+        greet(count - 1)
 
     label_load = pltpu.make_async_copy(regions, labels, load_sem.at[0])
 
@@ -143,6 +153,35 @@
                 )
             )
 
+    lanes = pl.ds((blocks - 1) * 128, 128)
+    short_copy = pltpu.make_async_remote_copy(
+        src_ref=adjoint.at[pl.ds(1, direct), far_row, :, lanes],
+        dst_ref=multipliers.at[(1 - odd) * (rows + 1), pl.ds(1, direct), :, lanes],
+        send_sem=far_send.at[1],
+        recv_sem=far_recv.at[blocks],
+        device_id={"space": outside},
+        device_id_type=MESH,
+    )
+    relay_out = [
+        pltpu.make_async_remote_copy(
+            src_ref=adjoint.at[pl.ds(1 + direct + d * carried, carried), far_row, :, lanes],
+            dst_ref=parcel,
+            send_sem=far_send.at[1],
+            recv_sem=relay_sem.at[0],
+            device_id={"space": jnp.int32(4 * (d + 1))},
+            device_id_type=MESH,
+        )
+        for d in range(relays)
+    ]
+    relay_on = pltpu.make_async_remote_copy(
+        src_ref=parcel,
+        dst_ref=multipliers.at[0, pl.ds(1 + direct + (link - 1) * carried, carried), :, lanes],
+        send_sem=relay_sem.at[1],
+        recv_sem=relay_sem.at[2],
+        device_id={"space": jnp.int32(0)},
+        device_id_type=MESH,
+    )
+
     def message(n, source, into, other):
         return pltpu.make_async_remote_copy(
             src_ref=source, dst_ref=into, send_sem=sum_send.at[n], recv_sem=sum_recv.at[n],
@@ -216,8 +255,8 @@
 
     @pl.when(last)
     def _():
-        pl.semaphore_wait(barrier, 3 + len(peers))
-        for copy in far_copies:
+        pl.semaphore_wait(barrier, 3 + len(peers) + len(helpers))
+        for copy in relay_out + far_copies[:-1] + [short_copy]:
             copy.start()
 
     @pl.when(hub)
@@ -327,6 +366,11 @@
         for send in chain_sums:
             send.start()
 
+        @pl.when(relay)
+        def _():
+            arrive(parcel, relay_sem.at[0])
+            relay_on.start()
+
         @pl.when(jnp.logical_not(last | origin))
         def _():
             @pl.when(place == 3)
@@ -363,7 +407,15 @@
 
     def add_far(block):
         lanes = pl.ds(block * 128, 128)
-        far_copies[blocks + block].wait_recv()
+        if block < blocks - 1:
+            far_copies[blocks + block].wait_recv()
+        else:
+            pl.when(jnp.logical_not(origin))(far_copies[-1].wait_recv)
+
+            @pl.when(origin)
+            def _():
+                short_copy.wait_recv()
+                arrive(multipliers.at[0, pl.ds(1 + direct, relays * carried), :, lanes], relay_sem.at[2])
 
         values = [-time_step * multipliers[far_halo, j + 1, :, lanes] for j in range(steps - 1)]
         values.append(jnp.zeros_like(values[0]))
@@ -382,6 +434,10 @@
     add_far(blocks - 1)
 
     arrive(multipliers.at[far_halo, pl.ds(1, steps - 1)], far_send.at[1])
+
+    @pl.when(relay)
+    def _():
+        arrive(parcel, relay_sem.at[1])
 
     @pl.when(hub)
     def _():
@@ -420,6 +476,7 @@
         + [vmem(padded, f32)] * 6
         + [
             vmem((count // 4 - 1,) + padded, f32),
+            vmem((RELAY_STEPS, planes, 128), f32),
             dma((7,)),
             pltpu.SemaphoreType.REGULAR,
             dma((2,)),
@@ -429,6 +486,7 @@
             dma((3,)),
             dma((3,)),
             dma((2,)),
+            dma((3,)),
         ],
         compiler_params=pltpu.CompilerParams(
             collective_id=0, has_side_effects=True, vmem_limit_bytes=24 * 2**20

time: 18.9 us -> 18.4 us (0.974)
  Pallas kernels: 18.1 us -> 17.6 us
    pallas_call x1, Pallas kernels: 15.7 us -> 15.2 us  [solve(): pl.pallas_call(functools.partial(solve_kernel, count), out_shape=(vmem((2...]
where the time goes in v2:
time: 18.4 us; the launch traced here: 18.2 us
  Pallas kernels  17.6 us (96%)
  between operations  0.64 us (3%)
    pallas_call x1, Pallas kernels, solve(): pl.pallas_call(functools.partial(solve_kernel, count), out_shape=(vmem((2...  15.2 us
    pallas_call x1, Pallas kernels, finish(): pl.pallas_call(finish_kernel, out_shape=(spectrum_shape, spectrum_shape,...  2.35 us

profile of v2, /device:TPU:1, one launch (start us, length us, event | category | flops | bytes accessed | tf_op | source)
XLA Modules:
  0.0 18.2 jit_solution(18044269643702928684)
XLA Ops:
  0.6 15.2 %solve.1 = (f32[2,32,4,8,256]{4,3,2,1,0:T(8,128)S(1)}, f32[4,32,8,256]{3,2,1,0:T(8,128)S(1)}, f32[32,4,8,256]{3,2,1,0:T(8,128)S(1)}, f32[32,128]{1,0:T(8,128)S(1)}, s32[4,8,256]{2,1,0:T(8,128)S(1)}) custom-call(f32[33,4,8,256]{3,2,1,0:T(8,128)} %state.1, f32[32,4,8,256]{3,2,1,0:T(8,128)} %adjoint.1, f32[32,4,8,256]{3,2,1,0:T(8,128)} %control.1, ...), custom_call_target="tpu_custom_call" | custom-call | tf_op jit(solution)/shard_map/solve/pallas_call | solution.py:456
  15.9 2.3 %finish.1 = (f32[2,32,4,8,256]{4,3,2,1,0:T(8,128)}, f32[2,32,4,8,256]{4,3,2,1,0:T(8,128)}, f32[32,4,8,256]{3,2,1,0:T(8,128)}) custom-call(f32[2,32,4,8,256]{4,3,2,1,0:T(8,128)S(1)} %get-tuple-element.8.state_buffer, f32[4,32,8,256]{3,2,1,0:T(8,128)S(1)} %get-tuple-element.9.packed, f32[32,4,8,256]{3,2,1,0:T(8,128)S(1)} %get-tuple-element.10.gradient, ...), custom_call_target="tpu_custom_call" | custom-call | tf_op jit(solution)/shard_map/finish/pallas_call | solution.py:547

commit v3 on v2

--- a/solution.py
+++ b/solution.py
@@ -58,10 +58,17 @@
     return real + [value for value in imag if value is not None]
 
 
+def halo_transform(multipliers, halo, lanes):
+    steps = multipliers.shape[1]
+    values = [-time_step * multipliers[halo, j + 1, :, lanes] for j in range(steps - 1)]
+    values.append(jnp.zeros_like(values[0]))
+    return pack(*real_transform(values))
+
+
 def solve_kernel(
     count, state, adjoint, control, regions, target, mask,
-    state_buffer, packed, gradient, misfit, labels,
-    sampled, held, multipliers, heat, wanted, allowed, residual, partial, paired, joined, crossed, summed, total, gathered, parcel,
+    state_buffer, packed, gradient, misfit, labels, multipliers,
+    sampled, held, heat, wanted, allowed, residual, partial, paired, joined, crossed, summed, total, gathered, parcel,
     load_sem, ready, near_send, near_recv, far_send, far_recv, sum_send, sum_recv, chain_sem, relay_sem,
 ):
     steps, rows, planes, width = control.shape
@@ -183,6 +190,7 @@
     )
 
     def message(n, source, into, other):
+        source, into = source.at[pl.ds(0, steps + 1)], into.at[pl.ds(0, steps + 1)]
         return pltpu.make_async_remote_copy(
             src_ref=source, dst_ref=into, send_sem=sum_send.at[n], recv_sem=sum_recv.at[n],
             device_id={"space": other}, device_id_type=MESH,
@@ -193,7 +201,7 @@
     share_sums = message(2, total, total, partner)
     chain_sums = [
         pltpu.make_async_remote_copy(
-            src_ref=summed, dst_ref=gathered.at[d], send_sem=chain_sem.at[0], recv_sem=chain_sem.at[1],
+            src_ref=summed.at[pl.ds(0, steps + 1)], dst_ref=gathered.at[d, pl.ds(0, steps + 1)], send_sem=chain_sem.at[0], recv_sem=chain_sem.at[1],
             device_id={"space": peer}, device_id_type=MESH,
         )
         for d, peer in enumerate(peers)
@@ -373,15 +381,18 @@
 
         @pl.when(jnp.logical_not(last | origin))
         def _():
-            @pl.when(place == 3)
+            @pl.when(place == 0)
             def _():
-                for copy in far_copies[:blocks]:
+                for copy in far_copies[blocks:]:
                     copy.start()
 
-            for copy in far_copies[blocks:]:
-                copy.start()
-
     lax.fori_loop(1, rows - 1, state_row, 0)
+
+    @pl.when((place == 3) & jnp.logical_not(last))
+    def _():
+        for copy in far_copies:
+            copy.start()
+
 
     for copy in near_copies:
         copy.wait()
@@ -396,7 +407,7 @@
     @pl.when(hub)
     def _():
         result = summed[...]
-        arrive(gathered, chain_sem.at[1])
+        arrive(gathered.at[:, pl.ds(0, steps + 1)], chain_sem.at[1])
         for d in range(len(peers)):
             result = result + gathered[d]
         total[...] = result
@@ -417,10 +428,9 @@
                 short_copy.wait_recv()
                 arrive(multipliers.at[0, pl.ds(1 + direct, relays * carried), :, lanes], relay_sem.at[2])
 
-        values = [-time_step * multipliers[far_halo, j + 1, :, lanes] for j in range(steps - 1)]
-        values.append(jnp.zeros_like(values[0]))
-        for k, value in enumerate(pack(*real_transform(values))):
-            packed[far_row, k, :, lanes] += value
+        if block < blocks - 1:
+            for k, value in enumerate(halo_transform(multipliers, far_halo, lanes)):
+                packed[far_row, k, :, lanes] += value
 
     for block in range(blocks - 1):
         add_far(block)
@@ -442,7 +452,7 @@
     @pl.when(hub)
     def _():
         arrive(held.at[far_halo, pl.ds(0, steps)], far_send.at[0])
-        arrive(gathered, chain_sem.at[0])
+        arrive(gathered.at[:, pl.ds(0, steps + 1)], chain_sem.at[0])
         share_sums.wait_send()
 
 
@@ -461,13 +471,13 @@
             vmem(control.shape, f32),
             vmem(target.shape, f32),
             vmem(regions.shape, jnp.int32),
+            vmem((rows + 2, steps, planes, width), f32),
         ),
         in_specs=[HBM] * 6,
-        out_specs=(in_vmem,) * 5,
+        out_specs=(in_vmem,) * 6,
         scratch_shapes=[
             vmem((rows, planes, steps, width), f32),
             vmem((rows + 2, steps + 1, planes, width), f32),
-            vmem((rows + 2, steps, planes, width), f32),
             vmem((rows, steps, planes, width), f32),
             vmem(target.shape, f32),
             pltpu.SMEM(mask.shape, jnp.int32),
@@ -496,9 +506,9 @@
 
 
 def finish_kernel(
-    state_buffer, packed, gradient, misfit, labels,
+    state_buffer, packed, gradient, misfit, labels, multipliers,
     state_out, adjoint_out, gradient_out,
-    adjoint_buffer, table, out_sem,
+    adjoint_buffer, table, late, out_sem,
 ):
     steps, rows, planes, width = gradient.shape
     writes = [
@@ -512,14 +522,25 @@
     for k, value in enumerate(pack(*values)):
         table[k] = value
 
+    blocks = width // 128
+    odd = lax.axis_index("space") % 2
+    for k, value in enumerate(
+        halo_transform(multipliers, odd * (rows + 1), pl.ds((blocks - 1) * 128, 128))
+    ):
+        late[0, k] = jnp.zeros_like(value)
+        late[1, k] = value
+
     def row_body(y, carry):
-        for block in range(width // 128):
+        chosen = jnp.where(y == odd * (rows - 1), 1, 0)
+        for block in range(blocks):
             lanes = pl.ds(block * 128, 128)
             ids = labels[y, :, lanes]
             values = [
                 packed[y, k, :, lanes] + jnp.take_along_axis(table[k], ids, axis=1, mode="promise_in_bounds")
                 for k in range(steps)
             ]
+            if block == blocks - 1:
+                values = [value + late[chosen, k] for k, value in enumerate(values)]
             top = steps // 2 + 1
             imag = [None] + values[top:] + [None] * (2 * top - 1 - steps)
 
@@ -539,7 +560,7 @@
     pltpu.make_async_copy(adjoint_buffer, adjoint_buffer, out_sem.at[2]).wait()
 
 
-def finish(control, state_buffer, packed, gradient, misfit, labels):
+def finish(control, state_buffer, packed, gradient, misfit, labels, multipliers):
     steps, rows, planes, width = control.shape
     f32, dma = jnp.float32, pltpu.SemaphoreType.DMA
     in_vmem = pl.BlockSpec(memory_space=pltpu.VMEM)
@@ -547,16 +568,17 @@
     return pl.pallas_call(
         finish_kernel,
         out_shape=(spectrum_shape, spectrum_shape, jax.ShapeDtypeStruct(control.shape, f32)),
-        in_specs=[in_vmem] * 5,
+        in_specs=[in_vmem] * 6,
         out_specs=(HBM,) * 3,
         scratch_shapes=[
             pltpu.VMEM((2, rows, steps, planes, width), f32),
             pltpu.VMEM((steps, 8, misfit.shape[1]), f32),
+            pltpu.VMEM((2, steps, planes, 128), f32),
             dma((3,)),
         ],
         compiler_params=pltpu.CompilerParams(vmem_limit_bytes=16 * 2**20),
         name="finish",
-    )(state_buffer, packed, gradient, misfit, labels)
+    )(state_buffer, packed, gradient, misfit, labels, multipliers)
 
 
 def on_device(count, *arrays):

time: 18.4 us -> 18.4 us (level)
  no operation moved by 1% of the time
where the time goes in v3:
time: 18.4 us; the launch traced here: 18.1 us
  Pallas kernels  17.5 us (95%)
  between operations  0.64 us (3%)
    pallas_call x1, Pallas kernels, solve(): pl.pallas_call(functools.partial(solve_kernel, count), out_shape=(vmem((2...  15.1 us
    pallas_call x1, Pallas kernels, finish(): pl.pallas_call(finish_kernel, out_shape=(spectrum_shape, spectrum_shape,...  2.35 us

profile of v3, /device:TPU:1, one launch (start us, length us, event | category | flops | bytes accessed | tf_op | source)
XLA Modules:
  0.0 18.1 jit_solution(18255200975341989332)
XLA Ops:
  0.6 15.1 %solve.1 = (f32[2,32,4,8,256]{4,3,2,1,0:T(8,128)S(1)}, f32[4,32,8,256]{3,2,1,0:T(8,128)S(1)}, f32[32,4,8,256]{3,2,1,0:T(8,128)S(1)}, f32[32,128]{1,0:T(8,128)S(1...) custom-call(f32[33,4,8,256]{3,2,1,0:T(8,128)} %state.1, f32[32,4,8,256]{3,2,1,0:T(8,128)} %adjoint.1, ...), custom_call_target="tpu_custom_call" | custom-call | tf_op jit(solution)/shard_map/solve/pallas_call | solution.py:466
  15.8 2.3 %finish.1 = (f32[2,32,4,8,256]{4,3,2,1,0:T(8,128)}, f32[2,32,4,8,256]{4,3,2,1,0:T(8,128)}, f32[32,4,8,256]{3,2,1,0:T(8,128)}) custom-call(f32[2,32,4,8,256]{4,3,2,1,0:T(8,128)S(1)} %get-tuple-element.9.state_buffer, f32[4,32,8,256]{3,2,1,0:T(8,128)S(1)} %get-tuple-element.10.packed, f32[32,4,8,256]{3,2,1,0:T(8,128)S(1)} %get-tuple-element.11.gradient, ...), custom_call_target="tpu_custom_call" | custom-call | tf_op jit(solution)/shard_map/finish/pallas_call | solution.py:568

commit v4 on v3

--- a/solution.py
+++ b/solution.py
@@ -69,7 +69,7 @@
     count, state, adjoint, control, regions, target, mask,
     state_buffer, packed, gradient, misfit, labels, multipliers,
     sampled, held, heat, wanted, allowed, residual, partial, paired, joined, crossed, summed, total, gathered, parcel,
-    load_sem, ready, near_send, near_recv, far_send, far_recv, sum_send, sum_recv, chain_sem, relay_sem,
+    load_sem, ready, near_sem, far_send, far_recv, sum_sem, chain_sem, relay_sem,
 ):
     steps, rows, planes, width = control.shape
     count_regions = target.shape[1]
@@ -116,20 +116,23 @@
         return pltpu.make_async_copy(source, into, sem)
 
     sample_loads = [
-        local(state.at[pl.ds(1, steps), y, plane], sampled.at[y, plane], load_sem.at[1])
+        local(state.at[pl.ds(1, steps), y, plane], sampled.at[y, plane], load_sem.at[0])
         for y in range(rows)
         for plane in range(planes)
     ]
-    later_loads = [local(target, wanted, load_sem.at[2]), local(mask, allowed, load_sem.at[3])]
+    later_loads = [local(mask, allowed, load_sem.at[1]), local(target, wanted, load_sem.at[2])]
     own = pl.ds(1, rows)
     for y in range(rows):
         later_loads += [
-            local(adjoint.at[pl.ds(0, steps), y], multipliers.at[y + 1], load_sem.at[4]),
-            local(control.at[pl.ds(0, steps), y], heat.at[y], load_sem.at[5]),
-            local(state.at[pl.ds(0, steps + 1), y], held.at[y + 1], load_sem.at[6]),
+            local(adjoint.at[pl.ds(0, steps), y], multipliers.at[y + 1], load_sem.at[3]),
+            local(control.at[pl.ds(0, steps), y], heat.at[y], load_sem.at[4]),
+            local(state.at[pl.ds(0, steps + 1), y], held.at[y + 1], load_sem.at[5]),
         ]
     def arrive(ref, sem):
         local(ref, ref, sem).wait()
+
+    def arrive_slabs(count, sem):
+        arrive(held.reshape((rows + 2) * (steps + 1), planes, width).at[pl.ds(0, count)], sem)
 
     near_copies, far_copies = [], []
     for source, first, target_rows, shift, length in (
@@ -140,8 +143,8 @@
             pltpu.make_async_remote_copy(
                 src_ref=source.at[pl.ds(first, length), near_row],
                 dst_ref=target_rows.at[odd * (rows + 1), pl.ds(shift, length)],
-                send_sem=near_send.at[n],
-                recv_sem=near_recv.at[n],
+                send_sem=near_sem.at[0],
+                recv_sem=near_sem.at[1],
                 device_id={"space": partner},
                 device_id_type=MESH,
             )
@@ -184,7 +187,7 @@
         src_ref=parcel,
         dst_ref=multipliers.at[0, pl.ds(1 + direct + (link - 1) * carried, carried), :, lanes],
         send_sem=relay_sem.at[1],
-        recv_sem=relay_sem.at[2],
+        recv_sem=relay_sem.at[0],
         device_id={"space": jnp.int32(0)},
         device_id_type=MESH,
     )
@@ -192,7 +195,7 @@
     def message(n, source, into, other):
         source, into = source.at[pl.ds(0, steps + 1)], into.at[pl.ds(0, steps + 1)]
         return pltpu.make_async_remote_copy(
-            src_ref=source, dst_ref=into, send_sem=sum_send.at[n], recv_sem=sum_recv.at[n],
+            src_ref=source, dst_ref=into, send_sem=sum_sem.at[0], recv_sem=sum_sem.at[1 + n % 2],
             device_id={"space": other}, device_id_type=MESH,
         )
 
@@ -242,8 +245,7 @@
         load.start()
     pl.when(place == 1)(meet)
 
-    label_load.wait()
-    arrive(sampled, load_sem.at[1])
+    arrive_slabs(rows * (steps + 1), load_sem.at[0])
     found = jnp.zeros((2 * steps + 16, count_regions), jnp.float32)
     for y in range(rows):
         found = add_row(y, found)
@@ -351,14 +353,13 @@
 
     for load in later_loads[:2]:
         load.wait()
-    arrive(multipliers.at[own], load_sem.at[4])
+    arrive(multipliers.at[own], load_sem.at[3])
+    arrive(heat, load_sem.at[4])
+    arrive(held.at[own], load_sem.at[5])
 
     lax.fori_loop(1, rows - 1, adjoint_full, 0)
 
     adjoint_transform(far_row, lambda j: multipliers[far_row + 2 - 2 * odd, j])
-
-    arrive(heat, load_sem.at[5])
-    arrive(held.at[own], load_sem.at[6])
 
     lax.fori_loop(0, rows, gradient_row, 0)
 
@@ -394,8 +395,8 @@
             copy.start()
 
 
-    for copy in near_copies:
-        copy.wait()
+    arrive_slabs(2 * steps - 1, near_sem.at[0])
+    arrive_slabs(2 * steps - 1, near_sem.at[1])
     lax.fori_loop(near_row, near_row + 1, adjoint_full, 0)
     lax.fori_loop(near_row, near_row + 1, state_row, 0)
 
@@ -426,7 +427,7 @@
             @pl.when(origin)
             def _():
                 short_copy.wait_recv()
-                arrive(multipliers.at[0, pl.ds(1 + direct, relays * carried), :, lanes], relay_sem.at[2])
+                arrive(multipliers.at[0, pl.ds(1 + direct, relays * carried), :, lanes], relay_sem.at[0])
 
         if block < blocks - 1:
             for k, value in enumerate(halo_transform(multipliers, far_halo, lanes)):
@@ -487,16 +488,14 @@
         + [
             vmem((count // 4 - 1,) + padded, f32),
             vmem((RELAY_STEPS, planes, 128), f32),
-            dma((7,)),
+            dma((6,)),
             pltpu.SemaphoreType.REGULAR,
-            dma((2,)),
             dma((2,)),
             dma((2,)),
             dma((1 + blocks,)),
             dma((3,)),
-            dma((3,)),
             dma((2,)),
-            dma((3,)),
+            dma((2,)),
         ],
         compiler_params=pltpu.CompilerParams(
             collective_id=0, has_side_effects=True, vmem_limit_bytes=24 * 2**20

time: 18.4 us -> 18.3 us (level)
  no operation moved by 1% of the time
where the time goes in v4:
time: 18.3 us; the launch traced here: 18.1 us
  Pallas kernels  17.4 us (95%)
  between operations  0.64 us (3%)
    pallas_call x1, Pallas kernels, solve(): pl.pallas_call(functools.partial(solve_kernel, count), out_shape=(vmem((2...  15.1 us
    pallas_call x1, Pallas kernels, finish(): pl.pallas_call(finish_kernel, out_shape=(spectrum_shape, spectrum_shape,...  2.35 us

profile of v4, /device:TPU:1, one launch (start us, length us, event | category | flops | bytes accessed | tf_op | source)
XLA Modules:
  0.0 18.1 jit_solution(12920819389312168631)
XLA Ops:
  0.6 15.1 %solve.1 = (f32[2,32,4,8,256]{4,3,2,1,0:T(8,128)S(1)}, f32[4,32,8,256]{3,2,1,0:T(8,128)S(1)}, f32[32,4,8,256]{3,2,1,0:T(8,128)S(1)}, f32[32,128]{1,0:T(8,128)S(1...) custom-call(f32[33,4,8,256]{3,2,1,0:T(8,128)} %state.1, f32[32,4,8,256]{3,2,1,0:T(8,128)} %adjoint.1, ...), custom_call_target="tpu_custom_call" | custom-call | tf_op jit(solution)/shard_map/solve/pallas_call | solution.py:467
  15.7 2.3 %finish.1 = (f32[2,32,4,8,256]{4,3,2,1,0:T(8,128)}, f32[2,32,4,8,256]{4,3,2,1,0:T(8,128)}, f32[32,4,8,256]{3,2,1,0:T(8,128)}) custom-call(f32[2,32,4,8,256]{4,3,2,1,0:T(8,128)S(1)} %get-tuple-element.9.state_buffer, f32[4,32,8,256]{3,2,1,0:T(8,128)S(1)} %get-tuple-element.10.packed, f32[32,4,8,256]{3,2,1,0:T(8,128)S(1)} %get-tuple-element.11.gradient, ...), custom_call_target="tpu_custom_call" | custom-call | tf_op jit(solution)/shard_map/finish/pallas_call | solution.py:567

commit v5 on v4

--- a/solution.py
+++ b/solution.py
@@ -12,7 +12,7 @@
 penalty = 0.5
 MESH = pl.DeviceIdType.MESH
 HBM = pl.BlockSpec(memory_space=pltpu.HBM)
-RELAY_STEPS = 4
+RELAY_STEPS = 5
 
 
 def real_transform(values):
@@ -185,7 +185,7 @@
     ]
     relay_on = pltpu.make_async_remote_copy(
         src_ref=parcel,
-        dst_ref=multipliers.at[0, pl.ds(1 + direct + (link - 1) * carried, carried), :, lanes],
+        dst_ref=multipliers.at[0, pl.ds(1 + direct + (link + relays - 1) % relays * carried, carried), :, lanes],
         send_sem=relay_sem.at[1],
         recv_sem=relay_sem.at[0],
         device_id={"space": jnp.int32(0)},

time: 18.3 us -> 18.2 us (level)
  no operation moved by 1% of the time
where the time goes in v5:
time: 18.2 us; the launch traced here: 18 us
  Pallas kernels  17.3 us (95%)
  between operations  0.64 us (4%)
    pallas_call x1, Pallas kernels, solve(): pl.pallas_call(functools.partial(solve_kernel, count), out_shape=(vmem((2...  15 us
    pallas_call x1, Pallas kernels, finish(): pl.pallas_call(finish_kernel, out_shape=(spectrum_shape, spectrum_shape,...  2.35 us

profile of v5, /device:TPU:1, one launch (start us, length us, event | category | flops | bytes accessed | tf_op | source)
XLA Modules:
  0.0 18.0 jit_solution(8355704637743332622)
XLA Ops:
  0.6 15.0 %solve.1 = (f32[2,32,4,8,256]{4,3,2,1,0:T(8,128)S(1)}, f32[4,32,8,256]{3,2,1,0:T(8,128)S(1)}, f32[32,4,8,256]{3,2,1,0:T(8,128)S(1)}, f32[32,128]{1,0:T(8,128)S(1...) custom-call(f32[33,4,8,256]{3,2,1,0:T(8,128)} %state.1, f32[32,4,8,256]{3,2,1,0:T(8,128)} %adjoint.1, ...), custom_call_target="tpu_custom_call" | custom-call | tf_op jit(solution)/shard_map/solve/pallas_call | solution.py:467
  15.6 2.3 %finish.1 = (f32[2,32,4,8,256]{4,3,2,1,0:T(8,128)}, f32[2,32,4,8,256]{4,3,2,1,0:T(8,128)}, f32[32,4,8,256]{3,2,1,0:T(8,128)}) custom-call(f32[2,32,4,8,256]{4,3,2,1,0:T(8,128)S(1)} %get-tuple-element.9.state_buffer, f32[4,32,8,256]{3,2,1,0:T(8,128)S(1)} %get-tuple-element.10.packed, f32[32,4,8,256]{3,2,1,0:T(8,128)S(1)} %get-tuple-element.11.gradient, ...), custom_call_target="tpu_custom_call" | custom-call | tf_op jit(solution)/shard_map/finish/pallas_call | solution.py:567

commit v6 on v5

--- a/solution.py
+++ b/solution.py
@@ -511,8 +511,8 @@
 ):
     steps, rows, planes, width = gradient.shape
     writes = [
+        pltpu.make_async_copy(gradient, gradient_out, out_sem.at[1]),
         pltpu.make_async_copy(state_buffer, state_out, out_sem.at[0]),
-        pltpu.make_async_copy(gradient, gradient_out, out_sem.at[1]),
     ]
     for write in writes:
         write.start()

time: 18.2 us -> 18.2 us (level)
  no operation moved by 1% of the time
where the time goes in v6:
time: 18.2 us; the launch traced here: 18 us
  Pallas kernels  17.3 us (95%)
  between operations  0.64 us (4%)
    pallas_call x1, Pallas kernels, solve(): pl.pallas_call(functools.partial(solve_kernel, count), out_shape=(vmem((2...  15 us
    pallas_call x1, Pallas kernels, finish(): pl.pallas_call(finish_kernel, out_shape=(spectrum_shape, spectrum_shape,...  2.34 us

profile of v6, /device:TPU:1, one launch (start us, length us, event | category | flops | bytes accessed | tf_op | source)
XLA Modules:
  0.0 18.0 jit_solution(15087443894626343158)
XLA Ops:
  0.6 15.0 %solve.1 = (f32[2,32,4,8,256]{4,3,2,1,0:T(8,128)S(1)}, f32[4,32,8,256]{3,2,1,0:T(8,128)S(1)}, f32[32,4,8,256]{3,2,1,0:T(8,128)S(1)}, f32[32,128]{1,0:T(8,128)S(1...) custom-call(f32[33,4,8,256]{3,2,1,0:T(8,128)} %state.1, f32[32,4,8,256]{3,2,1,0:T(8,128)} %adjoint.1, ...), custom_call_target="tpu_custom_call" | custom-call | tf_op jit(solution)/shard_map/solve/pallas_call | solution.py:467
  15.6 2.3 %finish.1 = (f32[2,32,4,8,256]{4,3,2,1,0:T(8,128)}, f32[2,32,4,8,256]{4,3,2,1,0:T(8,128)}, f32[32,4,8,256]{3,2,1,0:T(8,128)}) custom-call(f32[2,32,4,8,256]{4,3,2,1,0:T(8,128)S(1)} %get-tuple-element.9.state_buffer, f32[4,32,8,256]{3,2,1,0:T(8,128)S(1)} %get-tuple-element.10.packed, f32[32,4,8,256]{3,2,1,0:T(8,128)S(1)} %get-tuple-element.11.gradient, ...), custom_call_target="tpu_custom_call" | custom-call | tf_op jit(solution)/shard_map/finish/pallas_call | solution.py:567

commit v7 on v6

--- a/solution.py
+++ b/solution.py
@@ -143,8 +143,8 @@
             pltpu.make_async_remote_copy(
                 src_ref=source.at[pl.ds(first, length), near_row],
                 dst_ref=target_rows.at[odd * (rows + 1), pl.ds(shift, length)],
-                send_sem=near_sem.at[0],
-                recv_sem=near_sem.at[1],
+                send_sem=far_send.at[1],
+                recv_sem=near_sem.at[0],
                 device_id={"space": partner},
                 device_id_type=MESH,
             )
@@ -396,7 +396,6 @@
 
 
     arrive_slabs(2 * steps - 1, near_sem.at[0])
-    arrive_slabs(2 * steps - 1, near_sem.at[1])
     lax.fori_loop(near_row, near_row + 1, adjoint_full, 0)
     lax.fori_loop(near_row, near_row + 1, state_row, 0)
 
@@ -444,7 +443,7 @@
     misfit[...] = total[:steps] / total[steps : steps + 1] - wanted[...]
     add_far(blocks - 1)
 
-    arrive(multipliers.at[far_halo, pl.ds(1, steps - 1)], far_send.at[1])
+    arrive_slabs(3 * steps - 2, far_send.at[1])
 
     @pl.when(relay)
     def _():
@@ -490,7 +489,7 @@
             vmem((RELAY_STEPS, planes, 128), f32),
             dma((6,)),
             pltpu.SemaphoreType.REGULAR,
-            dma((2,)),
+            dma((1,)),
             dma((2,)),
             dma((1 + blocks,)),
             dma((3,)),

time: 18.2 us -> 18.2 us (level)
  no operation moved by 1% of the time
where the time goes in v7:
time: 18.2 us; the launch traced here: 18 us
  Pallas kernels  17.3 us (95%)
  between operations  0.64 us (4%)
    pallas_call x1, Pallas kernels, solve(): pl.pallas_call(functools.partial(solve_kernel, count), out_shape=(vmem((2...  15 us
    pallas_call x1, Pallas kernels, finish(): pl.pallas_call(finish_kernel, out_shape=(spectrum_shape, spectrum_shape,...  2.34 us

profile of v7, /device:TPU:1, one launch (start us, length us, event | category | flops | bytes accessed | tf_op | source)
XLA Modules:
  0.0 18.0 jit_solution(3955250191637909719)
XLA Ops:
  0.6 15.0 %solve.1 = (f32[2,32,4,8,256]{4,3,2,1,0:T(8,128)S(1)}, f32[4,32,8,256]{3,2,1,0:T(8,128)S(1)}, f32[32,4,8,256]{3,2,1,0:T(8,128)S(1)}, f32[32,128]{1,0:T(8,128)S(1...) custom-call(f32[33,4,8,256]{3,2,1,0:T(8,128)} %state.1, f32[32,4,8,256]{3,2,1,0:T(8,128)} %adjoint.1, ...), custom_call_target="tpu_custom_call" | custom-call | tf_op jit(solution)/shard_map/solve/pallas_call | solution.py:466
  15.6 2.3 %finish.1 = (f32[2,32,4,8,256]{4,3,2,1,0:T(8,128)}, f32[2,32,4,8,256]{4,3,2,1,0:T(8,128)}, f32[32,4,8,256]{3,2,1,0:T(8,128)}) custom-call(f32[2,32,4,8,256]{4,3,2,1,0:T(8,128)S(1)} %get-tuple-element.9.state_buffer, f32[4,32,8,256]{3,2,1,0:T(8,128)S(1)} %get-tuple-element.10.packed, f32[32,4,8,256]{3,2,1,0:T(8,128)S(1)} %get-tuple-element.11.gradient, ...), custom_call_target="tpu_custom_call" | custom-call | tf_op jit(solution)/shard_map/finish/pallas_call | solution.py:566
